TPU v7x, 32 devices: a whole 2x2x4 slice. The times are simulated.
32 devices in a mesh: band: 16 (over z, y, core), spin: 2 (over x).
Axes of the slice: x: 2, y: 2, z: 4, core: 2. Of those that a mesh axis runs over, the one named last changes fastest.
Arguments:
- coefficients: bfloat16 [2, 2, 32, 524288], P('spin', None, 'band'), may hold values from -1 to 1
- occupation: int32 [2, 32], P('spin', 'band'), may hold values from 0 to 1000
- miller: int32 [3, 524288], P(None, ('band', 'spin')), may hold values from -8 to 8
- density: float32 [2, 256, 128, 128], P('spin', 'band'), may hold values from 0.25 to 2
- local_factor: float32 [2, 256, 128, 128], P(None, None, 'band'), may hold values from -1.2 to 1.2
Outputs:
- stress: float32 [6], replicated
- kinetic_density: float32 [524288], P(('band', 'spin'))
- gradient_square: float32 [2, 256, 128, 128], P('spin', 'band')
All inputs are finite; a program needn't handle non-finite values.
Results may differ from a plain program's by a relative error of at most 0.0003.
Values sent between devices are 32-bit elements; how exact they have to be, the bound alone decides.
No kernel may reach another device: no remote copies, remote signals or barrier semaphores. Data moves between devices by JAX's collectives and lax.ppermute only.
A program may use at most 64 MiB of HBM per device.

v0:
```python
import jax
import jax.numpy as jnp
from jax import lax
from jax.sharding import PartitionSpec as P

NPW = 524288
NX = 128
NY = 128
NZ = 256
occupation_unit = 1000.0
kpoint = (0.25, 0.125, 0.375)
spacing = 0.25


def derivative_table(length):
    row_index = jnp.arange(length, dtype=jnp.int32)[:, None]
    col_index = jnp.arange(length, dtype=jnp.int32)[None, :]
    wrapped = jnp.mod(row_index - col_index, length)
    angles = jnp.pi / length * wrapped.astype(jnp.float32)
    on_diagonal = wrapped == 0
    sines = jnp.where(on_diagonal, 1.0, jnp.sin(angles))
    parity = 1.0 - 2.0 * jnp.mod(wrapped, 2).astype(jnp.float32)
    return jnp.where(on_diagonal, 0.0, 0.5 * parity * jnp.cos(angles) / sines)


def fourier_tables(length):
    positions = jnp.arange(length, dtype=jnp.int32)
    phases = jnp.mod(positions[:, None] * positions[None, :], length).astype(jnp.float32) * (
        2.0 * jnp.pi / length
    )
    return (jnp.cos(phases), jnp.sin(phases))


def frequencies(length):
    positions = jnp.arange(length, dtype=jnp.int32)
    signed = jnp.where(positions >= length // 2, positions - length, positions)
    return 2.0 * jnp.pi / length * signed.astype(jnp.float32)


def six_sums(weighting, first_axis, second_axis, third_axis):
    return jnp.stack(
        [
            jnp.sum(weighting * first_axis * first_axis),
            jnp.sum(weighting * second_axis * second_axis),
            jnp.sum(weighting * third_axis * third_axis),
            jnp.sum(weighting * second_axis * third_axis),
            jnp.sum(weighting * first_axis * third_axis),
            jnp.sum(weighting * first_axis * second_axis),
        ]
    )


def xc_terms(dens_part, grad_x, grad_y, grad_z, cell_count):
    square = grad_x * grad_x + grad_y * grad_y + grad_z * grad_z
    kernel = dens_part ** (-1.0 / 3.0) / (1.0 + square / (4.0 * dens_part * dens_part + 1.0))
    return (square, -six_sums(kernel, grad_x, grad_y, grad_z) / cell_count)


def shards(coefficients, occupation, miller, density, local_factor):
    highest = lax.Precision.HIGHEST
    weights = occupation.astype(jnp.float32) / occupation_unit
    piece = coefficients.astype(jnp.float32)
    squares = piece[0, 0] * piece[0, 0] + piece[0, 1] * piece[0, 1]
    kinetic_weight = lax.psum_scatter(
        jnp.dot(weights[0], squares, precision=highest),
        ("band", "spin"),
        scatter_dimension=0,
        tiled=True,
    )
    kvec = jnp.array(kpoint, jnp.float32)
    gvec = spacing * (miller.astype(jnp.float32) + kvec[:, None])
    kinetic_density = 0.5 * (gvec[0] ** 2 + gvec[1] ** 2 + gvec[2] ** 2) * kinetic_weight
    kinetic_stress = -six_sums(kinetic_weight, gvec[0], gvec[1], gvec[2]) / NPW
    band_devices = lax.axis_size("band")
    cell_count = density.shape[1] * band_devices * density.shape[2] * density.shape[3]
    deriv_x = derivative_table(NX)
    deriv_y = derivative_table(NY)
    deriv_z = derivative_table(NZ)
    cosine_x, sine_x = fourier_tables(NX)
    cosine_y, sine_y = fourier_tables(NY)
    cosine_z, sine_z = fourier_tables(NZ)
    grad_x = jnp.einsum("ik,szky->sziy", deriv_x, density, precision=highest)
    grad_y = jnp.einsum("ik,szxk->szxi", deriv_y, density, precision=highest)
    along_real = jnp.einsum("mj,szxj->szxm", cosine_y, density, precision=highest)
    along_imag = -jnp.einsum("mj,szxj->szxm", sine_y, density, precision=highest)
    plane_real = jnp.einsum("mj,szjy->szmy", cosine_x, along_real, precision=highest) + jnp.einsum(
        "mj,szjy->szmy", sine_x, along_imag, precision=highest
    )
    plane_imag = jnp.einsum("mj,szjy->szmy", cosine_x, along_imag, precision=highest) - jnp.einsum(
        "mj,szjy->szmy", sine_x, along_real, precision=highest
    )
    dens_col, real_col, imag_col = (
        lax.all_to_all(density, "band", split_axis=2, concat_axis=1, tiled=True),
        lax.all_to_all(plane_real, "band", split_axis=2, concat_axis=1, tiled=True),
        lax.all_to_all(plane_imag, "band", split_axis=2, concat_axis=1, tiled=True),
    )
    gradz_col = jnp.einsum("ik,skxy->sixy", deriv_z, dens_col, precision=highest)
    grad_z = lax.all_to_all(gradz_col, "band", split_axis=1, concat_axis=2, tiled=True)
    gradient_square, xc_stress = xc_terms(density, grad_x, grad_y, grad_z, cell_count)
    spec_real = (
        jnp.einsum("mj,jxy->mxy", cosine_z, real_col[0], precision=highest)
        + jnp.einsum("mj,jxy->mxy", sine_z, imag_col[0], precision=highest)
    ) / cell_count
    spec_imag = (
        jnp.einsum("mj,jxy->mxy", cosine_z, imag_col[0], precision=highest)
        - jnp.einsum("mj,jxy->mxy", sine_z, real_col[0], precision=highest)
    ) / cell_count
    total_real, total_imag = lax.psum((spec_real, spec_imag), "spin")
    local_rows = real_col.shape[2]
    first_column = lax.axis_index("band") * local_rows
    freq_z = frequencies(NZ)[:, None, None]
    freq_x = lax.dynamic_slice_in_dim(frequencies(NX), first_column, local_rows, 0)[None, :, None]
    freq_y = frequencies(NY)[None, None, :]
    length_sq = freq_x * freq_x + freq_y * freq_y + freq_z * freq_z
    positive = length_sq > 0
    inverse = jnp.where(positive, 1.0 / jnp.where(positive, length_sq, 1.0), 0.0)
    hartree_weight = 4.0 * jnp.pi * (total_real * total_real + total_imag * total_imag) * inverse
    diagonal = jnp.array([1.0, 1.0, 1.0, 0.0, 0.0, 0.0], jnp.float32)
    hartree_stress = 2.0 * six_sums(
        hartree_weight * inverse, freq_x, freq_y, freq_z
    ) - diagonal * jnp.sum(hartree_weight)
    local_weight = 2.0 * (total_real * local_factor[0] + total_imag * local_factor[1])
    local_stress = six_sums(local_weight, freq_x, freq_y, freq_z)
    spin_share = 1.0 / lax.axis_size("spin")
    partial_stress = kinetic_stress + spin_share * (hartree_stress + local_stress) + xc_stress
    stress = lax.psum(partial_stress, ("band", "spin"))
    return (stress, kinetic_density, gradient_square)


def solution(mesh):
    return jax.shard_map(
        shards,
        mesh=mesh,
        in_specs=(
            P("spin", None, "band", None),
            P("spin", "band"),
            P(None, ("band", "spin")),
            P("spin", "band", None, None),
            P(None, None, "band", None),
        ),
        out_specs=(P(), P(("band", "spin")), P("spin", "band", None, None)),
        check_vma=False,
    )
```

profile of v0, /device:TPU:0, one launch (start us, length us, event | category | flops | bytes accessed | tf_op | source)
XLA Modules:
  0.0 325.3 jit_solution(17758232457839028548)
XLA Ops:
  7.2 2.5 fusion.6
  9.7 2.5 convolution_bitcast_fusion.2
  16.1 7.5 %all-to-all-start.1 = ((f32[1,16,128,128]{3,1,0,2:T(8,128)}), f32[1,16,128,128]{3,1,0,2:T(8,128)}, u32[]{:S(2)}, u32[]{:S(2)}) async-start(f32[1,16,128,128]{3,1,0,2:T(8,128)} %copy.29), calls=%async_computation.1 | async-start | bytes 2097152 | tf_op jit(solution)/shard_map/all_to_all | solution.py:95
  24.0 4.7 %convert_element_type.102 = f32[1,2,2,524288]{3,2,1,0:T(2,128)S(1)} convert(bf16[1,2,2,524288]{3,2,1,0:T(2,128)(2,1)} %param.7) | non-fusion elementwise | flops 2097152 | bytes 12582912 | tf_op jit(solution)/shard_map/convert_element_type | solution.py:62
  28.7 17.0 %fusion.2 = f32[1,524288]{1,0:T(1,128)} fusion(f32[1,2,2,524288]{3,2,1,0:T(2,128)S(1)} %convert_element_type.102, s32[1,2]{1,0:T(1,128)S(1)} %copy-done.5), kind=kOutput, calls=%fused_computation.4 | convolution fusion | flops 15728644 | bytes 10485768 | tf_op jit(solution)/shard_map/dot_general | solution.py:65
  45.8 1.6 copy.35
  51.4 6.0 %all-to-all-start = ((f32[1,16,128,128]{3,1,0,2:T(8,128)}), f32[1,16,128,128]{3,1,0,2:T(8,128)S(1)}, u32[]{:S(2)}, u32[]{:S(2)}) async-start(f32[1,16,128,128]{3,1,0,2:T(8,128)} %copy.26), calls=%async_computation | async-start | bytes 2097152 | tf_op jit(solution)/shard_map/all_to_all | solution.py:94
  57.5 29.4 %all-to-all-done = f32[1,16,128,128]{3,1,0,2:T(8,128)S(1)} async-done(((f32[1,16,128,128]{3,1,0,2:T(8,128)}), f32[1,16,128,128]{3,1,0,2:T(8,128)S(1)}, u32[]{:S(2)}, u32[]{:S(2)}) %all-to-all-start) | async-done | bytes 1048608 | tf_op jit(solution)/shard_map/all_to_all | solution.py:94
  86.8 19.7 %all-to-all-start.2 = ((f32[1,16,128,128]{3,1,0,2:T(8,128)}), f32[1,16,128,128]{3,1,0,2:T(8,128)}, u32[]{:S(2)}, u32[]{:S(2)}) async-start(f32[1,16,128,128]{3,1,0,2:T(8,128)} %copy.35), calls=%async_computation.2 | async-start | bytes 2097152 | tf_op jit(solution)/shard_map/all_to_all | solution.py:93
  106.7 1.6 copy.59
  109.8 20.6 %all-to-all-done.2 = f32[1,16,128,128]{3,1,0,2:T(8,128)} async-done(((f32[1,16,128,128]{3,1,0,2:T(8,128)}), f32[1,16,128,128]{3,1,0,2:T(8,128)}, u32[]{:S(2)}, u32[]{:S(2)}) %all-to-all-start.2) | async-done | bytes 1048608 | tf_op jit(solution)/shard_map/all_to_all | solution.py:93
  131.7 2.2 convolution_bitcast_fusion
  134.0 1.6 copy.37
  135.6 6.9 %all-to-all-start.3 = ((f32[1,256,8,128]{3,2,0,1:T(8,128)}), f32[1,256,8,128]{3,2,0,1:T(8,128)}, u32[]{:S(2)}, u32[]{:S(2)}) async-start(f32[1,256,8,128]{3,2,0,1:T(8,128)} %copy.37), calls=%async_computation.3 | async-start | bytes 2097152 | tf_op jit(solution)/shard_map/all_to_all | solution.py:98
  142.5 2.0 fusion.45
  144.5 2.0 fusion.47
  146.5 3.1 fusion.7
  149.6 3.0 fusion.8
  152.7 2.3 convolution_bitcast_fusion.1
  155.1 1.7 fusion.203
  156.8 44.9 %all-reduce.5.cloned.1.call-done = f32[524288]{0:T(1024)} async-done(((f32[524288]{0:T(1024)}), f32[524288]{0:T(1024)}) %all-reduce.5.cloned.1.call-update) | async-done | bytes 2097168
  201.7 2.2 multiply_reduce_fusion.13
  203.9 3.7 %stack.90 = f32[6]{0:T(128)S(1)} concatenate(f32[1]{0:T(128)} %bitcast.5, f32[1]{0:T(128)} %bitcast.7, f32[1]{0:T(128)} %bitcast.9, f32[1]{0:T(128)} %bitcast.10, f32[1]{0:T(128)} %bitcast.11, f32[1]{0:T(128)} %bitcast.12), dimensions={0} | concatenate | bytes 48 | tf_op jit(solution)/shard_map/stack | solution.py:41
  207.7 5.9 %fusion.14 = (f32[1,16,128,128]{3,2,1,0:T(8,128)S(1)}, f32[1,16,128,128]{3,2,1,0:T(8,128)}, f32[128,16,128]{0,2,1:T(8,128)S(1)}) fusion(f32[1,16,128,128]{3,2,1,0:T(8,128)S(1)} %copy-done, f32[1,16,16,8,128]{4,3,2,1,0:T(8,128)} %bitcast.57, f32[1,16,128,128]{3,2,1,0:T(8,128)} %convolution_bitcast_fusion.1), kind=kOutput, calls=%fused_computation.27 | convolution fusion | flops 406093824 | bytes 6291456 | tf_op jit(solution)/shard_map/ik,szxk->szxi/dot_general | solution.py:83
  213.5 2.4 fusion.20
  216.0 3.8 %stack.111 = f32[6]{0:T(128)S(1)} concatenate(f32[1]{0:T(128)} %bitcast.60, f32[1]{0:T(128)} %bitcast.62, f32[1]{0:T(128)} %bitcast.64, f32[1]{0:T(128)} %bitcast.65, f32[1]{0:T(128)} %bitcast.66, f32[1]{0:T(128)} %bitcast.68), dimensions={0} | concatenate | bytes 48 | tf_op jit(solution)/shard_map/stack | solution.py:41
  219.8 46.0 %all-reduce.7.cloned.1.call-done = (f32[256,8,128]{2,0,1:T(8,128)}, f32[256,8,128]{2,0,1:T(8,128)}) async-done(((f32[256,8,128]{2,0,1:T(8,128)}, f32[256,8,128]{2,0,1:T(8,128)}), (f32[256,8,128]{2,0,1:T(8,128)}, f32[256,8,128]{2,0,1:T(8,128)})) %all-reduce.7.cloned.1.call-update) | async-done | bytes 2097168 | tf_op jit(solution)/shard_map/psum | solution.py:108
  265.9 2.8 fusion.121
  268.7 1.9 multiply_reduce_fusion.2
  270.6 3.8 %stack.97 = f32[6]{0:T(128)S(1)} concatenate(f32[1]{0:T(128)} %bitcast.30, f32[1]{0:T(128)} %bitcast.31, f32[1]{0:T(128)} %bitcast.32, f32[1]{0:T(128)} %bitcast.33, f32[1]{0:T(128)} %bitcast.34, f32[1]{0:T(128)} %bitcast.35), dimensions={0} | concatenate | bytes 48 | tf_op jit(solution)/shard_map/stack | solution.py:41
  274.4 3.8 %stack.104 = f32[6]{0:T(128)S(1)} concatenate(f32[1]{0:T(128)} %bitcast.38, f32[1]{0:T(128)} %bitcast.39, f32[1]{0:T(128)} %bitcast.40, f32[1]{0:T(128)} %bitcast.41, f32[1]{0:T(128)} %bitcast.42, f32[1]{0:T(128)} %bitcast.43), dimensions={0} | concatenate | bytes 48 | tf_op jit(solution)/shard_map/stack | solution.py:41
  278.9 39.3 %psum.23 = f32[6]{0:T(128)} all-reduce(f32[6]{0:T(128)S(1)} %multiply_add_fusion), channel_id=1, replica_groups=mesh['band'=16,'spin'=2] {'band','spin'}, use_global_device_ids=true, to_apply=%region_28.29 | all-reduce | flops 6 | bytes 48 | tf_op jit(solution)/shard_map/psum | solution.py:126
  (38 shorter events, 12.2 us)
Async XLA Ops:
  16.1 35.3 %all-to-all-start.1 = ((f32[1,16,128,128]{3,1,0,2:T(8,128)}), f32[1,16,128,128]{3,1,0,2:T(8,128)}, u32[]{:S(2)}, u32[]{:S(2)}) async-start(f32[1,16,128,128]{3,1,0,2:T(8,128)} %copy.29), calls=%async_computation.1 | async-start | bytes 2097152 | tf_op jit(solution)/shard_map/all_to_all | solution.py:95
  23.5 5.2 %copy-start.5 = (s32[1,2]{1,0:T(1,128)S(1)}, s32[1,2]{1,0:T(1,128)}, u32[]{:S(2)}) copy-start(s32[1,2]{1,0:T(1,128)} %param.8) | copy-start | bytes 28
  23.5 178.2 %all-reduce.5.cloned.1.call-start = ((), (), s32[]{:S(2)}) async-start(), calls=%async_computation.4 | async-start | bytes 4194304
  28.7 17.1 %copy-start = (f32[1,16,128,128]{3,2,1,0:T(8,128)S(1)}, f32[1,16,128,128]{3,2,1,0:T(8,128)}, u32[]{:S(2)}) copy-start(f32[1,16,128,128]{3,2,1,0:T(8,128)} %param.10) | copy-start | bytes 3145732
  48.6 8.7 %copy-start.2 = (s32[3,16384]{1,0:T(4,128)S(1)}, s32[3,16384]{1,0:T(4,128)}, u32[]{:S(2)}) copy-start(s32[3,16384]{1,0:T(4,128)} %param.9) | copy-start | bytes 589828
  48.6 8.7 %copy-start.3 = (f32[3]{0:T(128)S(1)}, f32[3]{0:T(128)}, u32[]{:S(2)}) copy-start(f32[3]{0:T(128)} %constant.139.clone) | copy-start | bytes 40
  51.4 35.5 %all-to-all-start = ((f32[1,16,128,128]{3,1,0,2:T(8,128)}), f32[1,16,128,128]{3,1,0,2:T(8,128)S(1)}, u32[]{:S(2)}, u32[]{:S(2)}) async-start(f32[1,16,128,128]{3,1,0,2:T(8,128)} %copy.26), calls=%async_computation | async-start | bytes 2097152 | tf_op jit(solution)/shard_map/all_to_all | solution.py:94
  86.8 43.6 %all-to-all-start.2 = ((f32[1,16,128,128]{3,1,0,2:T(8,128)}), f32[1,16,128,128]{3,1,0,2:T(8,128)}, u32[]{:S(2)}, u32[]{:S(2)}) async-start(f32[1,16,128,128]{3,1,0,2:T(8,128)} %copy.35), calls=%async_computation.2 | async-start | bytes 2097152 | tf_op jit(solution)/shard_map/all_to_all | solution.py:93
  135.6 72.1 %all-to-all-start.3 = ((f32[1,256,8,128]{3,2,0,1:T(8,128)}), f32[1,256,8,128]{3,2,0,1:T(8,128)}, u32[]{:S(2)}, u32[]{:S(2)}) async-start(f32[1,256,8,128]{3,2,0,1:T(8,128)} %copy.37), calls=%async_computation.3 | async-start | bytes 2097152 | tf_op jit(solution)/shard_map/all_to_all | solution.py:98
  142.4 123.4 %all-reduce.7.cloned.1.call-start = ((), (), s32[]{:S(2)}) async-start(), calls=%async_computation.5 | async-start | bytes 4194304 | tf_op jit(solution)/shard_map/psum | solution.py:108
  207.7 5.9 %copy-start.1 = (f32[1,16,128,128]{3,2,1,0:T(8,128)S(1)}, f32[1,16,128,128]{3,2,1,0:T(8,128)}, u32[]{:S(2)}) copy-start(f32[1,16,128,128]{3,2,1,0:T(8,128)} %convolution_bitcast_fusion.1) | copy-start | bytes 3145732
  265.8 12.4 %copy-start.4 = (f32[6]{0:T(128)S(1)}, f32[6]{0:T(128)}, u32[]{:S(2)}) copy-start(f32[6]{0:T(128)} %constant.140.clone) | copy-start | bytes 76
Sparse Core Ops, SparseCore 0:
  45.9 155.7 all-reduce.4
  204.1 61.7 all-reduce.6
where the time goes:
time: 331 us; the launch traced here: 325 us
  waiting for transfers between devices  141 us (43%)
  matrix products  47.5 us (14%)
  starting transfers between devices  40.4 us (12%)
  blocking collectives  39.3 us (12%)
  local copies, waits for them, and re-layouts  27.5 us (8%)
  other arithmetic  15.1 us (5%)
  between operations  14.5 us (4%)
    psum x1, waiting for transfers between devices, shards(): total_real, total_imag = lax.psum((spec_real, spec_imag), 'spin')  46 us
    unnamed x3, waiting for transfers between devices  45 us
    psum x1, blocking collectives, shards(): stress = lax.psum(partial_stress, ('band', 'spin'))  39.3 us
    all_to_all x1, waiting for transfers between devices, shards(): lax.all_to_all(plane_real, 'band', split_axis=2, concat_axis=1, tiled=True)  29.4 us
    all_to_all x1, waiting for transfers between devices, shards(): lax.all_to_all(density, 'band', split_axis=2, concat_axis=1, tiled=True)  20.6 us
    all_to_all x1, starting transfers between devices, shards(): lax.all_to_all(density, 'band', split_axis=2, concat_axis=1, tiled=True)  19.7 us
    dot_general x1, matrix products, shards(): jnp.dot(weights[0], squares, precision=highest)  17 us
    another operation x4, local copies, waits for them, and re-layouts, six_sums(): jnp.stack([jnp.sum(weighting * first_axis * first_axis), jnp.sum(weightin...  15.2 us
  transfers between devices with their start and end apart: 6, of which 4 were waited for; matrix products, arithmetic and copies ran while one was open for 21% of the time, Pallas kernels for 0%

commit v1 on v0

--- a/solution.py
+++ b/solution.py
@@ -91,7 +91,12 @@
     )
     dens_col, real_col, imag_col = (
         lax.all_to_all(density, "band", split_axis=2, concat_axis=1, tiled=True),
-        lax.all_to_all(plane_real, "band", split_axis=2, concat_axis=1, tiled=True),
+        jnp.concatenate(
+            lax.all_to_all(
+                jnp.stack(jnp.split(plane_real, lax.axis_size("band"), axis=2)), "band", 0, 0
+            ),
+            axis=1,
+        ),
         lax.all_to_all(plane_imag, "band", split_axis=2, concat_axis=1, tiled=True),
     )
     gradz_col = jnp.einsum("ik,skxy->sixy", deriv_z, dens_col, precision=highest)

time: 331 us -> 330 us (level)
  waiting for transfers between devices: 141 us -> 133 us
  local copies, waits for them, and re-layouts: 27.5 us -> 35 us
    all_to_all x1, starting transfers between devices: 19.7 us -> 5.96 us  [shards(): lax.all_to_all(density, 'band', split_axis=2, concat_axis=1, tiled=True)]
    all_to_all x1, starting transfers between devices: 5.96 us -> 18.3 us  [shards(): lax.all_to_all(jnp.stack(jnp.split(plane_real, lax.axis_size('band'), axi...]
    all_to_all x1, waiting for transfers between devices: 29.4 us -> 17.1 us  [shards(): lax.all_to_all(jnp.stack(jnp.split(plane_real, lax.axis_size('band'), axi...]
    unnamed x13 -> x32, local copies, waits for them, and re-layouts: 1.61 us -> 12 us
    all_to_all x1, waiting for transfers between devices: 20.6 us -> 26.3 us  [shards(): lax.all_to_all(density, 'band', split_axis=2, concat_axis=1, tiled=True)]
  transfers between devices with their start and end apart: 6 -> 6, of which waited for: 4 -> 4; matrix products, arithmetic and copies ran while one was open for 21% -> 23% of each run, Pallas kernels for 0% -> 0%
where the time goes in v1:
time: 330 us; the launch traced here: 324 us
  waiting for transfers between devices  133 us (40%)
  matrix products  47.7 us (14%)
  starting transfers between devices  39.4 us (12%)
  blocking collectives  39.3 us (12%)
  local copies, waits for them, and re-layouts  35 us (11%)
  other arithmetic  15.1 us (5%)
  between operations  14.5 us (4%)
    psum x1, waiting for transfers between devices, shards(): total_real, total_imag = lax.psum((spec_real, spec_imag), 'spin')  46 us
    unnamed x3, waiting for transfers between devices  43.7 us
    psum x1, blocking collectives, shards(): stress = lax.psum(partial_stress, ('band', 'spin'))  39.3 us
    all_to_all x1, waiting for transfers between devices, shards(): lax.all_to_all(density, 'band', split_axis=2, concat_axis=1, tiled=True)  26.3 us
    all_to_all x1, starting transfers between devices, shards(): lax.all_to_all(jnp.stack(jnp.split(plane_real, lax.axis_size('band'), axi...  18.3 us
    all_to_all x1, waiting for transfers between devices, shards(): lax.all_to_all(jnp.stack(jnp.split(plane_real, lax.axis_size('band'), axi...  17.1 us
    dot_general x1, matrix products, shards(): jnp.dot(weights[0], squares, precision=highest)  17 us
    another operation x4, local copies, waits for them, and re-layouts, six_sums(): jnp.stack([jnp.sum(weighting * first_axis * first_axis), jnp.sum(weightin...  15.2 us
  transfers between devices with their start and end apart: 6, of which 4 were waited for; matrix products, arithmetic and copies ran while one was open for 23% of the time, Pallas kernels for 0%

profile of v1, /device:TPU:0, one launch (start us, length us, event | category | flops | bytes accessed | tf_op | source)
XLA Modules:
  0.0 324.1 jit_solution(8679854039511306622)
XLA Ops:
  7.2 2.5 convolution_bitcast_fusion.2
  9.7 2.5 fusion.6
  16.1 7.5 %all-to-all-start.1 = ((f32[1,16,128,128]{3,1,0,2:T(8,128)}), f32[1,16,128,128]{3,1,0,2:T(8,128)}, u32[]{:S(2)}, u32[]{:S(2)}) async-start(f32[1,16,128,128]{3,1,0,2:T(8,128)} %copy.34), calls=%async_computation.1 | async-start | bytes 2097152 | tf_op jit(solution)/shard_map/all_to_all | solution.py:100
  24.0 4.7 %convert_element_type.102 = f32[1,2,2,524288]{3,2,1,0:T(2,128)S(1)} convert(bf16[1,2,2,524288]{3,2,1,0:T(2,128)(2,1)} %param.7) | non-fusion elementwise | flops 2097152 | bytes 12582912 | tf_op jit(solution)/shard_map/convert_element_type | solution.py:62
  28.7 17.0 %fusion.2 = f32[1,524288]{1,0:T(1,128)} fusion(f32[1,2,2,524288]{3,2,1,0:T(2,128)S(1)} %convert_element_type.102, s32[1,2]{1,0:T(1,128)S(1)} %copy-done.7), kind=kOutput, calls=%fused_computation.4 | convolution fusion | flops 15728644 | bytes 10485768 | tf_op jit(solution)/shard_map/dot_general | solution.py:65
  47.1 1.6 copy.41
  60.0 6.0 %all-to-all-start.2 = ((f32[1,16,128,128]{3,1,0,2:T(8,128)}), f32[1,16,128,128]{3,1,0,2:T(8,128)S(1)}, u32[]{:S(2)}, u32[]{:S(2)}) async-start(f32[1,16,128,128]{3,1,0,2:T(8,128)} %copy.41), calls=%async_computation.2 | async-start | bytes 2097152 | tf_op jit(solution)/shard_map/all_to_all | solution.py:93
  66.1 26.3 %all-to-all-done.2 = f32[1,16,128,128]{3,1,0,2:T(8,128)S(1)} async-done(((f32[1,16,128,128]{3,1,0,2:T(8,128)}), f32[1,16,128,128]{3,1,0,2:T(8,128)S(1)}, u32[]{:S(2)}, u32[]{:S(2)}) %all-to-all-start.2) | async-done | bytes 1048608 | tf_op jit(solution)/shard_map/all_to_all | solution.py:93
  93.4 18.3 %all-to-all-start = ((f32[16,1,16,8,128]{4,3,2,1,0:T(8,128)}), f32[16,1,16,8,128]{4,3,2,1,0:T(8,128)S(1)}, u32[]{:S(2)}, u32[]{:S(2)}) async-start(f32[16,1,16,8,128]{4,3,2,1,0:T(8,128)} %fusion.96), calls=%async_computation | async-start | bytes 2097152 | tf_op jit(solution)/shard_map/all_to_all | solution.py:95
  111.9 1.6 copy.70
  114.3 2.2 convolution_bitcast_fusion
  116.5 1.6 copy.43
  118.1 17.1 %all-to-all-done = f32[16,1,16,8,128]{4,3,2,1,0:T(8,128)S(1)} async-done(((f32[16,1,16,8,128]{4,3,2,1,0:T(8,128)}), f32[16,1,16,8,128]{4,3,2,1,0:T(8,128)S(1)}, u32[]{:S(2)}, u32[]{:S(2)}) %all-to-all-start) | async-done | bytes 1048608 | tf_op jit(solution)/shard_map/all_to_all | solution.py:95
  135.2 7.3 %all-to-all-start.3 = ((f32[1,256,8,128]{3,2,0,1:T(8,128)}), f32[1,256,8,128]{3,2,0,1:T(8,128)}, u32[]{:S(2)}, u32[]{:S(2)}) async-start(f32[1,256,8,128]{3,2,0,1:T(8,128)} %copy.43), calls=%async_computation.3 | async-start | bytes 2097152 | tf_op jit(solution)/shard_map/all_to_all | solution.py:103
  142.5 2.1 fusion.30
  144.6 2.0 fusion.48
  146.6 3.0 fusion.8
  149.7 3.1 fusion.7
  152.9 2.3 convolution_bitcast_fusion.1
  155.2 1.7 fusion.221
  156.9 43.6 %all-reduce.5.cloned.1.call-done = f32[524288]{0:T(1024)} async-done(((f32[524288]{0:T(1024)}), f32[524288]{0:T(1024)}) %all-reduce.5.cloned.1.call-update) | async-done | bytes 2097168
  200.6 2.2 multiply_reduce_fusion.13
  202.7 3.7 %stack.141 = f32[6]{0:T(128)S(1)} concatenate(f32[1]{0:T(128)} %bitcast.5, f32[1]{0:T(128)} %bitcast.7, f32[1]{0:T(128)} %bitcast.9, f32[1]{0:T(128)} %bitcast.10, f32[1]{0:T(128)} %bitcast.11, f32[1]{0:T(128)} %bitcast.12), dimensions={0} | concatenate | bytes 48 | tf_op jit(solution)/shard_map/stack | solution.py:41
  206.5 5.9 %fusion.14 = (f32[1,16,128,128]{3,2,1,0:T(8,128)S(1)}, f32[1,16,128,128]{3,2,1,0:T(8,128)}, f32[128,16,128]{0,2,1:T(8,128)S(1)}) fusion(f32[1,16,128,128]{3,2,1,0:T(8,128)S(1)} %copy-done, f32[1,16,16,8,128]{4,3,2,1,0:T(8,128)} %bitcast.72, f32[1,16,128,128]{3,2,1,0:T(8,128)} %convolution_bitcast_fusion.1), kind=kOutput, calls=%fused_computation.27 | convolution fusion | flops 406093824 | bytes 6291456 | tf_op jit(solution)/shard_map/ik,szxk->szxi/dot_general | solution.py:83
  212.3 2.4 fusion.20
  214.8 3.8 %stack.179 = f32[6]{0:T(128)S(1)} concatenate(f32[1]{0:T(128)} %bitcast.75, f32[1]{0:T(128)} %bitcast.77, f32[1]{0:T(128)} %bitcast.79, f32[1]{0:T(128)} %bitcast.80, f32[1]{0:T(128)} %bitcast.81, f32[1]{0:T(128)} %bitcast.83), dimensions={0} | concatenate | bytes 48 | tf_op jit(solution)/shard_map/stack | solution.py:41
  218.6 46.0 %all-reduce.7.cloned.1.call-done = (f32[256,8,128]{2,0,1:T(8,128)}, f32[256,8,128]{2,0,1:T(8,128)}) async-done(((f32[256,8,128]{2,0,1:T(8,128)}, f32[256,8,128]{2,0,1:T(8,128)}), (f32[256,8,128]{2,0,1:T(8,128)}, f32[256,8,128]{2,0,1:T(8,128)})) %all-reduce.7.cloned.1.call-update) | async-done | bytes 2097168 | tf_op jit(solution)/shard_map/psum | solution.py:113
  264.7 2.8 fusion.139
  267.5 1.9 multiply_reduce_fusion.2
  269.4 3.8 %stack.165 = f32[6]{0:T(128)S(1)} concatenate(f32[1]{0:T(128)} %bitcast.45, f32[1]{0:T(128)} %bitcast.46, f32[1]{0:T(128)} %bitcast.47, f32[1]{0:T(128)} %bitcast.48, f32[1]{0:T(128)} %bitcast.49, f32[1]{0:T(128)} %bitcast.50), dimensions={0} | concatenate | bytes 48 | tf_op jit(solution)/shard_map/stack | solution.py:41
  273.2 3.8 %stack.172 = f32[6]{0:T(128)S(1)} concatenate(f32[1]{0:T(128)} %bitcast.53, f32[1]{0:T(128)} %bitcast.54, f32[1]{0:T(128)} %bitcast.55, f32[1]{0:T(128)} %bitcast.56, f32[1]{0:T(128)} %bitcast.57, f32[1]{0:T(128)} %bitcast.58), dimensions={0} | concatenate | bytes 48 | tf_op jit(solution)/shard_map/stack | solution.py:41
  277.7 39.3 %psum.23 = f32[6]{0:T(128)} all-reduce(f32[6]{0:T(128)S(1)} %multiply_add_fusion), channel_id=1, replica_groups=mesh['band'=16,'spin'=2] {'band','spin'}, use_global_device_ids=true, to_apply=%region_28.29 | all-reduce | flops 6 | bytes 48 | tf_op jit(solution)/shard_map/psum | solution.py:131
  (55 shorter events, 19.7 us)
Async XLA Ops:
  16.1 44.0 %all-to-all-start.1 = ((f32[1,16,128,128]{3,1,0,2:T(8,128)}), f32[1,16,128,128]{3,1,0,2:T(8,128)}, u32[]{:S(2)}, u32[]{:S(2)}) async-start(f32[1,16,128,128]{3,1,0,2:T(8,128)} %copy.34), calls=%async_computation.1 | async-start | bytes 2097152 | tf_op jit(solution)/shard_map/all_to_all | solution.py:100
  23.5 5.2 %copy-start.7 = (s32[1,2]{1,0:T(1,128)S(1)}, s32[1,2]{1,0:T(1,128)}, u32[]{:S(2)}) copy-start(s32[1,2]{1,0:T(1,128)} %param.8) | copy-start | bytes 28
  23.5 177.0 %all-reduce.5.cloned.1.call-start = ((), (), s32[]{:S(2)}) async-start(), calls=%async_computation.4 | async-start | bytes 4194304
  45.8 1.3 copy-start
  47.1 18.9 %copy-start.4 = (s32[3,16384]{1,0:T(4,128)S(1)}, s32[3,16384]{1,0:T(4,128)}, u32[]{:S(2)}) copy-start(s32[3,16384]{1,0:T(4,128)} %param.9) | copy-start | bytes 589828
  47.1 18.9 %copy-start.5 = (f32[3]{0:T(128)S(1)}, f32[3]{0:T(128)}, u32[]{:S(2)}) copy-start(f32[3]{0:T(128)} %constant.139.clone) | copy-start | bytes 40
  60.0 32.4 %all-to-all-start.2 = ((f32[1,16,128,128]{3,1,0,2:T(8,128)}), f32[1,16,128,128]{3,1,0,2:T(8,128)S(1)}, u32[]{:S(2)}, u32[]{:S(2)}) async-start(f32[1,16,128,128]{3,1,0,2:T(8,128)} %copy.41), calls=%async_computation.2 | async-start | bytes 2097152 | tf_op jit(solution)/shard_map/all_to_all | solution.py:93
  92.4 1.0 copy-start.1
  93.4 41.9 %all-to-all-start = ((f32[16,1,16,8,128]{4,3,2,1,0:T(8,128)}), f32[16,1,16,8,128]{4,3,2,1,0:T(8,128)S(1)}, u32[]{:S(2)}, u32[]{:S(2)}) async-start(f32[16,1,16,8,128]{4,3,2,1,0:T(8,128)} %fusion.96), calls=%async_computation | async-start | bytes 2097152 | tf_op jit(solution)/shard_map/all_to_all | solution.py:95
  111.8 2.4 copy-start.2
  135.2 71.3 %all-to-all-start.3 = ((f32[1,256,8,128]{3,2,0,1:T(8,128)}), f32[1,256,8,128]{3,2,0,1:T(8,128)}, u32[]{:S(2)}, u32[]{:S(2)}) async-start(f32[1,256,8,128]{3,2,0,1:T(8,128)} %copy.43), calls=%async_computation.3 | async-start | bytes 2097152 | tf_op jit(solution)/shard_map/all_to_all | solution.py:103
  142.5 122.2 %all-reduce.7.cloned.1.call-start = ((), (), s32[]{:S(2)}) async-start(), calls=%async_computation.5 | async-start | bytes 4194304 | tf_op jit(solution)/shard_map/psum | solution.py:113
  206.5 5.9 %copy-start.3 = (f32[1,16,128,128]{3,2,1,0:T(8,128)S(1)}, f32[1,16,128,128]{3,2,1,0:T(8,128)}, u32[]{:S(2)}) copy-start(f32[1,16,128,128]{3,2,1,0:T(8,128)} %convolution_bitcast_fusion.1) | copy-start | bytes 3145732
  264.7 12.4 %copy-start.6 = (f32[6]{0:T(128)S(1)}, f32[6]{0:T(128)}, u32[]{:S(2)}) copy-start(f32[6]{0:T(128)} %constant.140.clone) | copy-start | bytes 76
Sparse Core Ops, SparseCore 0:
  45.9 154.6 all-reduce.4
  202.9 61.7 all-reduce.6
